TPU v7x, 32 devices: a whole 2x2x4 slice. The times are simulated.
32 devices in a mesh: groups: 2 (over x), dev: 16 (over z, y, core).
Axes of the slice: x: 2, y: 2, z: 4, core: 2. Of those that a mesh axis runs over, the one named last changes fastest.
Arguments:
- queries: bfloat16 [32, 512, 512], P(('groups', 'dev')), parts along dimension 0, may hold values from -120 to 120
- key_values: bfloat16 [2, 32, 512, 128], P(None, ('groups', 'dev')), parts along dimension 1, may hold values from -4 to 4
- lengths: int32 [4], P('groups'), parts along dimension 0, may hold values from 1 to 512, as said below
- out_proj: bfloat16 [4096, 2048], P('dev'), may hold values from -0.09375 to 0.09375
- residual: bfloat16 [32, 64, 2048], P(('groups', 'dev')), parts along dimension 0, may hold values from -8 to 8
- norm_gain: bfloat16 [2048], replicated, may hold values from 0.25 to 1.75
- router: bfloat16 [2048, 16], replicated, may hold values from -0.125 to 0.125
- expert_ids: int32 [32, 64, 8], P(('groups', 'dev')), parts along dimension 0, may hold values from 0 to 15, all different within a row; in each aligned block of 64 rows (0 to 63, 64 to 127, ..., all dimensions but the last counted through in order) at most 48 rows name the same one
- expert_gate_up: bfloat16 [16, 2048, 1536], P('dev'), may hold values from -0.125 to 0.125
- expert_down: bfloat16 [16, 768, 2048], P('dev'), may hold values from -0.21875 to 0.21875
Outputs:
- output: bfloat16 [32, 64, 2048], P(('groups', 'dev')), parts along dimension 0
There are 2 independent parts, one for each index of `groups`. A program takes and returns all parts, laid end to end along the dimension named above; an argument that names none is the same for every part. Nothing has to cross between parts.
Inputs may be any that keep to these rules, and one draw needn't show every extreme that they name: `lengths`: in every draw some request has all 512 cache slots filled. Each token names 8 different experts. The tokens of one block of expert_ids name any one expert at most 48 times, and in every draw some block names some expert exactly 48 times.
All inputs are finite; a program needn't handle non-finite values.
Results may differ from a plain program's by a relative error of at most 0.011.
Values may be sent and summed in bfloat16 or wider, within the bound.
A program may use at most 128 MiB of HBM per device.

v0:
```python
import math

import jax
import jax.numpy as jnp
from jax import lax
from jax.sharding import PartitionSpec as P

D = 2048
HEAD_DIM = 128
FF = 768
TOP = 8
TOK_DEV = 64
CTX = 512
GROUP = 8
QH = 4
SPAN = 512


EPSILON = 1e-06


def partner(block, axis, stride):
    count = lax.axis_size(axis)
    route = []
    for low in range(count):
        high = low | 1 << stride
        if high != low and high < count:
            route += [(low, high), (high, low)]
    return lax.ppermute(block, axis, route)


def bit_count(number):
    return number.bit_length() - 1


def per_device(
    queries,
    key_values,
    lengths,
    out_proj,
    residual,
    norm_gain,
    router,
    expert_ids,
    expert_gate_up,
    expert_down,
):
    devices = lax.axis_size("dev")
    my_index = lax.axis_index("dev")
    requests_n = devices // GROUP
    low_bits = bit_count(requests_n)
    tp_rank = my_index // requests_n
    request = my_index % requests_n
    is_upper = tp_rank % 2 == 1
    own_half = key_values[:, 0]
    other_half = partner(own_half, "dev", low_bits)
    first_part = jnp.where(is_upper, other_half, own_half)
    second_part = jnp.where(is_upper, own_half, other_half)
    key_seq = jnp.concatenate([first_part, second_part], axis=1)
    length = lengths[request]
    positions = jnp.arange(CTX + SPAN, dtype=jnp.int32)
    qblock = math.gcd(SPAN, 256)
    score_scale = 1.0 / math.sqrt(HEAD_DIM)
    block_queries = queries[0].reshape(SPAN // qblock, qblock, QH, HEAD_DIM)
    starts = jnp.arange(SPAN // qblock, dtype=jnp.int32) * qblock

    def attend(element):
        block_q, start = element
        scores = (
            jnp.einsum("tjd,pd->jtp", block_q, key_seq[0], preferred_element_type=jnp.float32)
            * score_scale
        )
        row_ids = start + jnp.arange(qblock, dtype=jnp.int32)
        visible = (positions[None, :] < length) | (positions[None, :] >= CTX) & (
            positions[None, :] - CTX <= row_ids[:, None]
        )
        scores = jnp.where(visible[None], scores, -jnp.inf)
        row_max = jnp.max(scores, axis=-1, keepdims=True)
        raised = jnp.exp(scores - row_max)
        weights = (raised / jnp.sum(raised, axis=-1, keepdims=True)).astype(jnp.bfloat16)
        mixture = jnp.einsum("jtp,pd->tjd", weights, key_seq[1], preferred_element_type=jnp.float32)
        return mixture.astype(jnp.bfloat16)

    head_out = lax.map(attend, (block_queries, starts)).reshape(SPAN, QH * HEAD_DIM)
    proj_block = out_proj
    for bit_no in range(low_bits):
        arrived = partner(proj_block, "dev", bit_no)
        is_high = my_index >> bit_no & 1 == 1
        proj_block = jnp.where(
            is_high,
            jnp.concatenate([arrived, proj_block], axis=0),
            jnp.concatenate([proj_block, arrived], axis=0),
        )
    partial_value = jnp.dot(head_out, proj_block, preferred_element_type=jnp.float32)
    rank_bits = bit_count(GROUP)
    pieces = partial_value.reshape((2,) * rank_bits + (TOK_DEV, D))
    live_bits = list(range(rank_bits - 1, -1, -1))
    order_bits = list(range(rank_bits - 1, -1, -1))
    for bit_no in order_bits:
        axis_no = live_bits.index(bit_no)
        my_bit = tp_rank >> bit_no & 1
        kept_half = lax.dynamic_index_in_dim(pieces, my_bit, axis_no, keepdims=False)
        sent_half = lax.dynamic_index_in_dim(pieces, 1 - my_bit, axis_no, keepdims=False)
        pieces = kept_half + partner(sent_half, "dev", low_bits + bit_no)
        live_bits.pop(axis_no)
    stream = (residual[0].astype(jnp.float32) + pieces).astype(jnp.bfloat16)
    values = stream.astype(jnp.float32)
    normed = (
        values
        * lax.rsqrt(jnp.mean(values * values, axis=-1, keepdims=True) + EPSILON)
        * norm_gain.astype(jnp.float32)
    ).astype(jnp.bfloat16)
    logits = jnp.dot(normed, router, preferred_element_type=jnp.float32)
    experts_n = router.shape[1]
    token_ids = expert_ids[0]
    onehot = token_ids[..., None] == jnp.arange(experts_n, dtype=jnp.int32)
    chosen = jnp.sum(jnp.where(onehot, logits[:, None, :], 0.0), axis=-1)
    raised_gate = jnp.exp(chosen)
    gate_weights = raised_gate / jnp.sum(raised_gate, axis=-1, keepdims=True)
    flat_marks = onehot.reshape(TOK_DEV * TOP, experts_n).astype(jnp.int32)
    before = jnp.cumsum(flat_marks, axis=0) - flat_marks
    slot_index = jnp.sum(before * flat_marks, axis=1)
    flat_ids = token_ids.reshape(-1)
    capacity = max(2, 3 * TOK_DEV * TOP // (2 * devices))
    send_rows = flat_ids * capacity + slot_index
    outbound = (
        jnp.zeros((experts_n * capacity, D), jnp.bfloat16)
        .at[send_rows]
        .set(jnp.repeat(normed, TOP, axis=0))
    )
    outbound = outbound.reshape(experts_n, capacity, D)
    routed = lax.all_to_all(outbound, "dev", split_axis=0, concat_axis=0, tiled=True)
    sources = routed.shape[0]
    slots_each = routed.shape[1]
    flat_rows = routed.reshape(sources * slots_each, routed.shape[2])
    projected = jnp.dot(flat_rows, expert_gate_up[0], preferred_element_type=jnp.float32)
    activation = (jax.nn.silu(projected[:, :FF]) * projected[:, FF:]).astype(jnp.bfloat16)
    produced = jnp.dot(activation, expert_down[0], preferred_element_type=jnp.float32).astype(
        jnp.bfloat16
    )
    computed = produced.reshape(sources, slots_each, produced.shape[1])
    returned = lax.all_to_all(computed, "dev", split_axis=0, concat_axis=0, tiled=True)
    results = returned.reshape(experts_n * capacity, D)[send_rows].reshape(TOK_DEV, TOP, D)
    combined = jnp.sum(gate_weights[:, :, None] * results, axis=1)
    return (values + combined).astype(jnp.bfloat16)[None]


def solution(mesh):
    return jax.shard_map(
        per_device,
        mesh=mesh,
        in_specs=(
            P(("groups", "dev"), None, None),
            P(None, ("groups", "dev"), None, None),
            P("groups"),
            P("dev", None),
            P(("groups", "dev"), None, None),
            P(),
            P(),
            P(("groups", "dev"), None, None),
            P("dev", None, None),
            P("dev", None, None),
        ),
        out_specs=P(("groups", "dev"), None, None),
        check_vma=False,
    )
```

profile of v0, /device:TPU:13, one launch (start us, length us, event | category | flops | bytes accessed | tf_op | source)
XLA Modules:
  0.0 366.2 jit_solution(15075617977227872624)
XLA Ops:
  1.2 2.0 reshape_squeeze.4
  4.5 2.9 collective-permute-done
  9.2 24.7 %while.14 = (s32[]{:T(128)}, bf16[2,256,4,128]{3,2,1,0:T(4,128)(2,1)}, s32[]{:T(128)}, s32[2]{0:T(128)S(1)}, bf16[2,256,4,128]{3,2,1,0:T(4,128)(2,1)}, /*index=5*/bf16[2,1024,128]{2,1,0:T(8,128)(2,1)}, s32[]{:T(128)}) while((s32[]{:T(128)}, bf16[2,256,4,128]{3,2,1,0:T(4,128)(2,1)}, s32[]{:T(128)}, s32[2]{0:T(128)S(1)}, ...), condition=%wide.region_3.4_spmd.clone.clone, body=%wide.region_0.3_spmd.clone.clone.sunk | while | flops 544084224 | bytes 11033189 | solution.py:84
  13.2 4.5 %fusion.79 = (f32[4,256]{1,0:T(4,128)S(1)}, f32[4,256,1024]{2,1,0:T(8,128)}) fusion(pred[256,1024]{1,0:T(8,128)(4,1)} %and_or_fusion.2, bf16[1,256,4,128]{3,2,1,0:T(4,128)(2,1)S(1)} %constant_dynamic-slice_fusion.2, bf16[2,1024,128]{2,1,0:T(8,128)(2,1)} %get-tuple-element.230), kind=kOutput, calls=%fused_computation.95.clone.1 | convolution fusion | flops 272630784 | bytes 4984832 | tf_op jit(solution)/shard_map/while/body/eval_jaxpr/sub | solution.py:79
  17.7 3.0 fusion.80
  25.6 4.5 %fusion.79 = (f32[4,256]{1,0:T(4,128)S(1)}, f32[4,256,1024]{2,1,0:T(8,128)}) fusion(pred[256,1024]{1,0:T(8,128)(4,1)} %and_or_fusion.2, bf16[1,256,4,128]{3,2,1,0:T(4,128)(2,1)S(1)} %constant_dynamic-slice_fusion.2, bf16[2,1024,128]{2,1,0:T(8,128)(2,1)} %get-tuple-element.230), kind=kOutput, calls=%fused_computation.95.clone.1 | convolution fusion | flops 272630784 | bytes 4984832 | tf_op jit(solution)/shard_map/while/body/eval_jaxpr/sub | solution.py:79
  30.1 3.0 fusion.80
  34.0 2.0 dot_general.20
  36.0 3.7 %fusion.36 = f32[2,2,2,64,2048]{4,3,2,1,0:T(8,128)S(1)} fusion(bf16[2,2,2,64,512]{4,3,2,1,0:T(8,128)(2,1)} %dot_general.20, bf16[256,2048]{1,0:T(8,128)(2,1)} %param.15, bf16[256,2048]{1,0:T(8,128)(2,1)} %collective-permute-done.1, pred[]{:T(512)S(6)} %eq.44), kind=kOutput, calls=%fused_computation.44 | convolution fusion | flops 1083179008 | bytes 6815745 | tf_op jit(solution)/shard_map/dot_general | solution.py:94
  39.8 1.9 copy-done.2
  43.2 2.3 collective-permute-start.2
  45.5 90.5 %collective-permute-done.2 = f32[2,2,64,2048]{3,2,1,0:T(8,128)} collective-permute-done((f32[2,2,64,2048]{3,2,1,0:T(8,128)}, f32[2,2,64,2048]{3,2,1,0:T(8,128)}, u32[]{:S(2)}, u32[]{:S(2)}) %collective-permute-start.2) | collective-permute-done | bytes 2097184 | tf_op jit(solution)/shard_map/ppermute | solution.py:29
  136.0 2.5 bitcast_add_fusion
  142.6 22.8 %collective-permute-done.3 = f32[2,64,2048]{2,1,0:T(8,128)} collective-permute-done((f32[2,64,2048]{2,1,0:T(8,128)}, f32[2,64,2048]{2,1,0:T(8,128)}, u32[]{:S(2)}, u32[]{:S(2)}) %collective-permute-start.3) | collective-permute-done | bytes 1048608 | tf_op jit(solution)/shard_map/ppermute | solution.py:29
  165.4 1.7 bitcast_add_fusion.1
  169.4 11.9 %collective-permute-done.4 = f32[64,2048]{1,0:T(8,128)} collective-permute-done((f32[64,2048]{1,0:T(8,128)}, f32[64,2048]{1,0:T(8,128)}, u32[]{:S(2)}, u32[]{:S(2)}) %collective-permute-start.4) | collective-permute-done | bytes 524320 | tf_op jit(solution)/shard_map/ppermute | solution.py:29
  183.6 5.7 %scatter_custom_fusion = bf16[768,2048]{1,0:T(8,128)(2,1)} fusion(s32[512]{0:T(512)S(1)} %bitcast.133, bf16[]{:T(256)} %constant.108.clone.1, bf16[64,2048]{1,0:T(8,128)(2,1)S(1)} %fusion.52), kind=kCustom, calls=%fused_computation.50 | custom fusion | bytes 3407874 | tf_op jit(solution)/shard_map/scatter | solution.py:129
  189.3 78.6 %all_to_all.10 = bf16[16,48,2048]{2,1,0:T(8,128)(2,1)S(1)} all-to-all(bf16[16,48,2048]{2,1,0:T(8,128)(2,1)} %bitcast.128), channel_id=1, replica_groups=mesh['groups'=2,'dev'=16] {'dev'}, dimensions={0} | all-to-all | bytes 6291456 | tf_op jit(solution)/shard_map/all_to_all | solution.py:132
  267.8 7.1 %fusion.30 = f32[768,1536]{1,0:T(8,128)S(1)} fusion(bf16[768,2048]{1,0:T(8,128)(2,1)S(1)} %bitcast.130, bf16[1,2048,1536]{2,1,0:T(8,128)(2,1)} %param.20), kind=kOutput, calls=%fused_computation.34 | convolution fusion | flops 4831838208 | bytes 14155776 | tf_op jit(solution)/shard_map/dot_general | solution.py:136
  275.0 4.1 %convolution_convert_fusion = bf16[768,2048]{1,0:T(8,128)(2,1)} fusion(bf16[1,768,2048]{2,1,0:T(8,128)(2,1)S(1)} %copy-done, f32[768,1536]{1,0:T(8,128)S(1)} %fusion.30), kind=kOutput, calls=%fused_computation.38 | convolution fusion | flops 2421030912 | bytes 11010048 | tf_op jit(solution)/shard_map/dot_general | solution.py:138
  279.1 5.2 %all-to-all-start.1 = ((bf16[16,48,2048]{2,1,0:T(8,128)(2,1)}), bf16[16,48,2048]{2,1,0:T(8,128)(2,1)}, u32[]{:S(2)}, u32[]{:S(2)}) async-start(bf16[16,48,2048]{2,1,0:T(8,128)(2,1)} %bitcast.129), calls=%async_computation.1 | async-start | bytes 6291456 | tf_op jit(solution)/shard_map/all_to_all | solution.py:142
  284.7 69.6 %all-to-all-done.1 = bf16[16,48,2048]{2,1,0:T(8,128)(2,1)} async-done(((bf16[16,48,2048]{2,1,0:T(8,128)(2,1)}), bf16[16,48,2048]{2,1,0:T(8,128)(2,1)}, u32[]{:S(2)}, u32[]{:S(2)}) %all-to-all-start.1) | async-done | bytes 3145760 | tf_op jit(solution)/shard_map/all_to_all | solution.py:142
  354.4 7.6 %gather_fusion = bf16[512,2048]{1,0:T(8,128)(2,1)} fusion(bf16[768,2048]{1,0:T(8,128)(2,1)} %bitcast.21, s32[1024]{0:T(1024)S(1)} %pad_clamp_fusion), kind=kCustom, calls=%fused_computation | custom fusion | bytes 4196352 | tf_op jit(solution)/shard_map/gather | solution.py:143
  361.9 3.4 fusion.32
  (70 shorter events, 25.4 us)
Async XLA Ops:
  0.0 275.0 %copy-start = (bf16[1,768,2048]{2,1,0:T(8,128)(2,1)S(1)}, bf16[1,768,2048]{2,1,0:T(8,128)(2,1)}, u32[]{:S(2)}) copy-start(bf16[1,768,2048]{2,1,0:T(8,128)(2,1)} %param.21) | copy-start | bytes 9437188
  0.0 7.4 %collective-permute-start = (bf16[2,512,128]{2,1,0:T(8,128)(2,1)}, bf16[2,512,128]{2,1,0:T(8,128)(2,1)S(1)}, u32[]{:S(2)}, u32[]{:S(2)}) collective-permute-start(bf16[2,512,128]{2,1,0:T(8,128)(2,1)} %bitcast.131), channel_id=1, source_target_pairs={{0,2},{2,0},{1,3},{3,1},{4,6},{6,4},{5,7},{7,5},{8,10},{10,8},{9,1... | collective-permute-start | bytes 786440 | tf_op jit(solution)/shard_map/ppermute | solution.py:29
  0.2 35.8 %collective-permute-start.1 = (bf16[256,2048]{1,0:T(8,128)(2,1)}, bf16[256,2048]{1,0:T(8,128)(2,1)}, u32[]{:S(2)}, u32[]{:S(2)}) collective-permute-start(bf16[256,2048]{1,0:T(8,128)(2,1)} %param.15), channel_id=1, source_target_pairs={{0,1},{1,0},{2,3},{3,2},{4,5},{5,4},{6,7},{7,6},{8,9},{9,8},{10,11... | collective-permute-start | bytes 3145736 | tf_op jit(solution)/shard_map/ppermute | solution.py:29
  39.7 1.9 copy-start.2
  43.2 92.8 %collective-permute-start.2 = (f32[2,2,64,2048]{3,2,1,0:T(8,128)}, f32[2,2,64,2048]{3,2,1,0:T(8,128)}, u32[]{:S(2)}, u32[]{:S(2)}) collective-permute-start(f32[2,2,64,2048]{3,2,1,0:T(8,128)} %dynamic-slice_bitcast_fusion), channel_id=1, source_target_pairs={{0,8},{8,0},{1,9},{9,1},{2,10},{10,2},{3,11},{11,3},{4,12},{12,4},... | collective-permute-start | bytes 6291464 | tf_op jit(solution)/shard_map/ppermute | solution.py:29
  45.5 95.5 %copy-start.8 = (s32[1,64,8]{1,2,0:T(8,128)S(1)}, s32[1,64,8]{1,2,0:T(8,128)}, u32[]{:S(2)}) copy-start(s32[1,64,8]{1,2,0:T(8,128)} %param.19) | copy-start | bytes 6148
  45.5 95.7 %copy-start.9 = (bf16[2048]{0:T(1024)(128)(2,1)S(1)}, bf16[2048]{0:T(1024)(128)(2,1)}, u32[]{:S(2)}) copy-start(bf16[2048]{0:T(1024)(128)(2,1)} %param.17) | copy-start | bytes 12292
  138.4 1.4 copy-start.1
  139.8 41.5 %copy-start.6 = (bf16[1,64,2048]{2,1,0:T(8,128)(2,1)S(1)}, bf16[1,64,2048]{2,1,0:T(8,128)(2,1)}, u32[]{:S(2)}) copy-start(bf16[1,64,2048]{2,1,0:T(8,128)(2,1)} %param.16) | copy-start | bytes 786436
  140.8 24.5 %collective-permute-start.3 = (f32[2,64,2048]{2,1,0:T(8,128)}, f32[2,64,2048]{2,1,0:T(8,128)}, u32[]{:S(2)}, u32[]{:S(2)}) collective-permute-start(f32[2,64,2048]{2,1,0:T(8,128)} %dynamic-slice_bitcast_fusion.1), channel_id=1, source_target_pairs={{0,4},{4,0},{1,5},{5,1},{2,6},{6,2},{3,7},{7,3},{8,12},{12,8},{9,1... | collective-permute-start | bytes 3145736 | tf_op jit(solution)/shard_map/ppermute | solution.py:29
  167.0 1.0 copy-start.3
  168.9 12.4 %collective-permute-start.4 = (f32[64,2048]{1,0:T(8,128)}, f32[64,2048]{1,0:T(8,128)}, u32[]{:S(2)}, u32[]{:S(2)}) collective-permute-start(f32[64,2048]{1,0:T(8,128)} %dynamic-slice_bitcast_fusion.2), channel_id=1, source_target_pairs={{0,2},{2,0},{1,3},{3,1},{4,6},{6,4},{5,7},{7,5},{8,10},{10,8},{9,1... | collective-permute-start | bytes 1572872 | tf_op jit(solution)/shard_map/ppermute | solution.py:29
  182.7 0.7 copy-start.4
  279.1 5.3 %copy-start.7 = (bf16[2048,16]{0,1:T(8,128)(2,1)S(1)}, bf16[2048,16]{0,1:T(8,128)(2,1)}, u32[]{:S(2)}) copy-start(bf16[2048,16]{0,1:T(8,128)(2,1)} %param.18) | copy-start | bytes 196612
  279.1 75.2 %all-to-all-start.1 = ((bf16[16,48,2048]{2,1,0:T(8,128)(2,1)}), bf16[16,48,2048]{2,1,0:T(8,128)(2,1)}, u32[]{:S(2)}, u32[]{:S(2)}) async-start(bf16[16,48,2048]{2,1,0:T(8,128)(2,1)} %bitcast.129), calls=%async_computation.1 | async-start | bytes 6291456 | tf_op jit(solution)/shard_map/all_to_all | solution.py:142
  354.4 11.0 %copy-start.5 = (bf16[64,2048]{1,0:T(8,128)(2,1)S(1)}, bf16[64,2048]{1,0:T(8,128)(2,1)}, u32[]{:S(2)}) copy-start(bf16[64,2048]{1,0:T(8,128)(2,1)} %copy-done.4) | copy-start | bytes 786436
where the time goes:
time: 367 us; the launch traced here: 366 us
  waiting for transfers between devices  198 us (54%)
  blocking collectives  78.6 us (21%)
  local copies, waits for them, and re-layouts  32.8 us (9%)
  matrix products  30.1 us (8%)
  other arithmetic  17.7 us (5%)
  starting transfers between devices  9.02 us (2%)
    ppermute x5, waiting for transfers between devices, partner(): return lax.ppermute(block, axis, route)  128 us
    all_to_all x1, blocking collectives, per_device(): lax.all_to_all(outbound, 'dev', split_axis=0, concat_axis=0, tiled=True)  78.6 us
    all_to_all x1, waiting for transfers between devices, per_device(): lax.all_to_all(computed, 'dev', split_axis=0, concat_axis=0, tiled=True)  69.6 us
    sub x2, matrix products, attend(): raised = jnp.exp(scores - row_max)  8.98 us
    gather x1, local copies, waits for them, and re-layouts, per_device(): returned.reshape(experts_n * capacity, D)[send_rows]  7.57 us
  transfers between devices with their start and end apart: 6, of which 5 were waited for; matrix products, arithmetic and copies ran while one was open for 9% of the time, Pallas kernels for 0%

commit v1 on v0

v1 whole, which is shorter than its diff:
```python
import functools
import math

import jax
import jax.numpy as jnp
from jax import lax
from jax.experimental import pallas as pl
from jax.experimental.pallas import tpu as pltpu
from jax.sharding import PartitionSpec as P

HEAD_DIM = 128
FF = 768
TOP = 8
TOK_DEV = 64
CTX = 512
GROUP = 8
QH = 4
SPAN = 512
EPSILON = 1e-06
MESH = pl.DeviceIdType.MESH


def bit_count(number):
    return number.bit_length() - 1


def flipped(index, bits):
    for bit in bits:
        index = index + (1 - 2 * ((index // (1 << bit)) % 2)) * (1 << bit)
    return index


def subset(bits, number):
    return [bit for place, bit in enumerate(bits) if number >> place & 1]


def greet(me, bits):
    barrier = pltpu.get_barrier_semaphore()
    for bit in bits:
        pl.semaphore_signal(
            barrier, inc=1, device_id={"dev": flipped(me, [bit])}, device_id_type=MESH
        )
    pl.semaphore_wait(barrier, len(bits))


def scatter_steps(me, unit, part_no, order, cols, x_ref, recv, stage, send_sem, recv_sem, block_of):
    k = len(order)
    total = (1 << k) - 1
    first = [total - ((1 << (k - s)) - 1) for s in range(k)]

    def arrived(step, number):
        return pltpu.make_async_remote_copy(
            src_ref=recv.at[first[step] + number, :, cols],
            dst_ref=recv.at[first[step] + number, :, cols],
            send_sem=send_sem.at[part_no, first[step] + number],
            recv_sem=recv_sem.at[part_no, first[step] + number],
            device_id={"dev": flipped(me, [unit + order[step]])},
            device_id_type=MESH,
        )

    copies = []

    def send(step):
        for number in range(1 << (k - 1 - step)):
            slot = first[step] + number
            flips = [order[step]] + subset(order[step + 1 :], number)
            block = block_of(flips)
            if step == 0:
                source = x_ref.at[block, :, cols]
            else:
                value = x_ref[block, :, cols].astype(jnp.float32)
                for earlier in range(step):
                    place = (1 << (step - earlier - 1)) + (number << (step - earlier))
                    arrived(earlier, place).wait_recv()
                    value = value + recv[first[earlier] + place, :, cols].astype(jnp.float32)
                spot = slot - first[1]
                stage[spot, :, cols] = value.astype(stage.dtype)
                source = stage.at[spot, :, cols]
            copy = pltpu.make_async_remote_copy(
                src_ref=source,
                dst_ref=recv.at[slot, :, cols],
                send_sem=send_sem.at[part_no, slot],
                recv_sem=recv_sem.at[part_no, slot],
                device_id={"dev": flipped(me, [unit + order[step]])},
                device_id_type=MESH,
            )
            copy.start()
            copies.append(copy)

    def finish(o_ref):
        value = x_ref[block_of([]), :, cols].astype(jnp.float32)
        for earlier in range(k):
            arrived(earlier, 0).wait_recv()
            value = value + recv[first[earlier], :, cols].astype(jnp.float32)
        o_ref[:, cols] = value
        for copy in copies:
            copy.wait_send()

    return send, finish


def scatter_kernel(unit, parts, bits, x_ref, o_ref, recv, stage, send_sem, recv_sem):
    me = lax.axis_index("dev")
    greet(me, [unit + bit for bit in bits])
    rank = me // (1 << unit)
    runs = [
        scatter_steps(
            me, unit, number, order, cols, x_ref, recv, stage, send_sem, recv_sem,
            lambda flips: flipped(rank, flips),
        )
        for number, (order, cols) in enumerate(parts)
    ]
    for step in range(len(bits)):
        for send, _ in runs:
            send(step)
    for _, finish in runs:
        finish(o_ref)


def reduce_scatter(x, unit, orders, collective_id):
    blocks, rows, width = x.shape
    bits = sorted(orders[0])
    cut = width * 3 // 4 // 128 * 128
    parts = [(orders[0], pl.ds(0, cut)), (orders[1], pl.ds(cut, width - cut))]
    return pl.pallas_call(
        functools.partial(scatter_kernel, unit, parts, bits),
        out_shape=jax.ShapeDtypeStruct((rows, width), jnp.float32),
        in_specs=[pl.BlockSpec(memory_space=pltpu.VMEM)],
        out_specs=pl.BlockSpec(memory_space=pltpu.VMEM),
        scratch_shapes=[
            pltpu.VMEM((blocks - 1, rows, width), x.dtype),
            pltpu.VMEM((max(blocks // 2 - 1, 1), rows, width), x.dtype),
            pltpu.SemaphoreType.DMA((2, blocks - 1)),
            pltpu.SemaphoreType.DMA((2, blocks - 1)),
        ],
        compiler_params=pltpu.CompilerParams(collective_id=collective_id, has_side_effects=True),
    )(x)


def gather_kernel(parts, bits, x_ref, g_ref, ox_ref, og_ref, send_sem, recv_sem, own_sem):
    me = lax.axis_index("dev")
    greet(me, bits)
    k = len(bits)
    pairs = [(x_ref, ox_ref), (g_ref, og_ref)]
    local = []
    for number, (source, target) in enumerate(pairs):
        copy = pltpu.make_async_copy(source, target.at[me], own_sem.at[number])
        copy.start()
        local.append(copy)
    sent = []

    def forward(part_no, held, step):
        which, order, cols = parts[part_no]
        source, target = pairs[which]
        block = flipped(me, subset(order, held))
        slot = (1 << step) - 1 + held
        copy = pltpu.make_async_remote_copy(
            src_ref=source.at[:, cols] if held == 0 else target.at[block, :, cols],
            dst_ref=target.at[block, :, cols],
            send_sem=send_sem.at[part_no, slot],
            recv_sem=recv_sem.at[part_no, slot],
            device_id={"dev": flipped(me, [order[step]])},
            device_id_type=MESH,
        )
        copy.start()
        sent.append(copy)

    def arrive(part_no, held, step):
        which, order, cols = parts[part_no]
        target = pairs[which][1]
        block = flipped(me, subset(order, held) + [order[step]])
        slot = (1 << step) - 1 + held
        pltpu.make_async_remote_copy(
            src_ref=target.at[block, :, cols],
            dst_ref=target.at[block, :, cols],
            send_sem=send_sem.at[part_no, slot],
            recv_sem=recv_sem.at[part_no, slot],
            device_id={"dev": flipped(me, [order[step]])},
            device_id_type=MESH,
        ).wait_recv()

    for step in range(k):
        for part_no in range(len(parts)):
            forward(part_no, 0, step)
    for step in range(k):
        for held in range(1 << step):
            for part_no in range(len(parts)):
                arrive(part_no, held, step)
                for later in range(step + 1, k):
                    forward(part_no, held + (1 << step), later)
    for copy in local:
        copy.wait()
    for copy in sent:
        copy.wait_send()


def all_gather(x, gates, orders, collective_id):
    rows, width = x.shape
    bits = sorted(orders[0])
    count = 1 << len(bits)
    cut = width * 3 // 4 // 128 * 128
    parts = [
        (1, orders[0], pl.ds(0, gates.shape[1])),
        (0, orders[0], pl.ds(0, cut)),
        (0, orders[1], pl.ds(cut, width - cut)),
    ]
    return pl.pallas_call(
        functools.partial(gather_kernel, parts, bits),
        out_shape=[
            jax.ShapeDtypeStruct((count, rows, width), x.dtype),
            jax.ShapeDtypeStruct((count,) + gates.shape, gates.dtype),
        ],
        in_specs=[pl.BlockSpec(memory_space=pltpu.VMEM)] * 2,
        out_specs=[pl.BlockSpec(memory_space=pltpu.VMEM)] * 2,
        scratch_shapes=[
            pltpu.SemaphoreType.DMA((3, count - 1)),
            pltpu.SemaphoreType.DMA((3, count - 1)),
            pltpu.SemaphoreType.DMA((2,)),
        ],
        compiler_params=pltpu.CompilerParams(collective_id=collective_id, has_side_effects=True),
    )(x, gates)


def swapped(order, one, two):
    order = list(order)
    order[one], order[two] = order[two], order[one]
    return order


def partner(block, axis, stride):
    count = lax.axis_size(axis)
    route = [(i, i ^ 1 << stride) for i in range(count)]
    return lax.ppermute(block, axis, route)


def per_device(
    queries,
    key_values,
    lengths,
    out_proj,
    residual,
    norm_gain,
    router,
    expert_ids,
    expert_gate_up,
    expert_down,
):
    devices = lax.axis_size("dev")
    my_index = lax.axis_index("dev")
    width = residual.shape[-1]
    requests_n = devices // GROUP
    low_bits = bit_count(requests_n)
    tp_rank = my_index // requests_n
    request = my_index % requests_n
    is_upper = tp_rank % 2 == 1
    own_half = key_values[:, 0]
    other_half = partner(own_half, "dev", low_bits)
    first_part = jnp.where(is_upper, other_half, own_half)
    second_part = jnp.where(is_upper, own_half, other_half)
    key_seq = jnp.concatenate([first_part, second_part], axis=1)
    length = lengths[request]
    positions = jnp.arange(CTX + SPAN, dtype=jnp.int32)
    qblock = math.gcd(SPAN, 256)
    score_scale = 1.0 / math.sqrt(HEAD_DIM)
    block_queries = queries[0].reshape(SPAN // qblock, qblock, QH, HEAD_DIM)
    starts = jnp.arange(SPAN // qblock, dtype=jnp.int32) * qblock

    def attend(element):
        block_q, start = element
        scores = (
            jnp.einsum("tjd,pd->jtp", block_q, key_seq[0], preferred_element_type=jnp.float32)
            * score_scale
        )
        row_ids = start + jnp.arange(qblock, dtype=jnp.int32)
        visible = (positions[None, :] < length) | (positions[None, :] >= CTX) & (
            positions[None, :] - CTX <= row_ids[:, None]
        )
        scores = jnp.where(visible[None], scores, -jnp.inf)
        row_max = jnp.max(scores, axis=-1, keepdims=True)
        raised = jnp.exp(scores - row_max)
        weights = (raised / jnp.sum(raised, axis=-1, keepdims=True)).astype(jnp.bfloat16)
        mixture = jnp.einsum("jtp,pd->tjd", weights, key_seq[1], preferred_element_type=jnp.float32)
        return mixture.astype(jnp.bfloat16)

    head_out = lax.map(attend, (block_queries, starts)).reshape(SPAN, QH * HEAD_DIM)
    proj_block = out_proj
    for bit_no in range(low_bits):
        arrived = partner(proj_block, "dev", bit_no)
        is_high = my_index >> bit_no & 1 == 1
        proj_block = jnp.where(
            is_high,
            jnp.concatenate([arrived, proj_block], axis=0),
            jnp.concatenate([proj_block, arrived], axis=0),
        )
    partial_value = jnp.dot(head_out, proj_block, preferred_element_type=jnp.float32)
    pieces = partial_value.astype(jnp.bfloat16).reshape(GROUP, TOK_DEV, width)
    near = list(range(bit_count(GROUP)))
    attended = reduce_scatter(pieces, low_bits, [near, swapped(near, 0, 1)], 1)
    stream = (residual[0].astype(jnp.float32) + attended).astype(jnp.bfloat16)
    values = stream.astype(jnp.float32)
    normed = (
        values
        * lax.rsqrt(jnp.mean(values * values, axis=-1, keepdims=True) + EPSILON)
        * norm_gain.astype(jnp.float32)
    ).astype(jnp.bfloat16)
    logits = jnp.dot(normed, router, preferred_element_type=jnp.float32)
    experts_n = router.shape[1]
    token_ids = expert_ids[0]
    named = jnp.any(token_ids[..., None] == jnp.arange(experts_n, dtype=jnp.int32), axis=1)
    raised_gate = jnp.where(named, jnp.exp(logits), 0.0)
    gates = raised_gate / jnp.sum(raised_gate, axis=-1, keepdims=True)
    lanes = -(-TOK_DEV // 128) * 128
    gates = jnp.pad(gates.T, ((0, 0), (0, lanes - TOK_DEV)))
    every = list(range(bit_count(devices)))
    far = every[::-1]
    count = len(far)
    rows_all, gates_all = all_gather(normed, gates, [far, swapped(far, count - 3, count - 2)], 2)
    my_gates = lax.dynamic_index_in_dim(gates_all, my_index, 1, keepdims=False)[:, :TOK_DEV]
    flat_rows = rows_all.reshape(devices * TOK_DEV, width)
    projected = jnp.dot(flat_rows, expert_gate_up[0], preferred_element_type=jnp.float32)
    activation = (jax.nn.silu(projected[:, :FF]) * projected[:, FF:]).astype(jnp.bfloat16)
    produced = jnp.dot(activation, expert_down[0], preferred_element_type=jnp.float32)
    weighted = (my_gates.reshape(-1, 1) * produced).astype(jnp.bfloat16)
    weighted = weighted.reshape(devices, TOK_DEV, width)
    combined = reduce_scatter(weighted, 0, [every, swapped(every, 1, 2)], 3)
    return (values + combined).astype(jnp.bfloat16)[None]


def solution(mesh):
    return jax.shard_map(
        per_device,
        mesh=mesh,
        in_specs=(
            P(("groups", "dev"), None, None),
            P(None, ("groups", "dev"), None, None),
            P("groups"),
            P("dev", None),
            P(("groups", "dev"), None, None),
            P(),
            P(),
            P(("groups", "dev"), None, None),
            P("dev", None, None),
            P("dev", None, None),
        ),
        out_specs=P(("groups", "dev"), None, None),
        check_vma=False,
    )
```

time: 367 us -> 177 us (0.48)
  the two profiles are of different devices: /device:TPU:13 before, /device:TPU:0 now
where the time goes in v1:
time: 177 us
  Pallas kernels  114 us (64%)
  matrix products  35.5 us (20%)
  other arithmetic  10.9 us (6%)
  local copies, waits for them, and re-layouts  10.8 us (6%)
  starting transfers between devices  3 us (2%)
  waiting for transfers between devices  1.87 us (1%)
    pallas_call x2, Pallas kernels, reduce_scatter(): pl.pallas_call(functools.partial(scatter_kernel, unit, parts, bits), out_...  81.9 us
    pallas_call x1, Pallas kernels, all_gather(): pl.pallas_call(functools.partial(gather_kernel, parts, bits), out_shape=[...  32.6 us
    dot_general x1, matrix products, per_device(): jnp.dot(flat_rows, expert_gate_up[0], preferred_element_type=jnp.float32)  10 us
    sub x2, matrix products, attend(): raised = jnp.exp(scores - row_max)  9 us
    dot_general x2, matrix products, attend(): jnp.einsum('jtp,pd->tjd', weights, key_seq[1], preferred_element_type=jnp...  6.06 us
    dot_general x1, matrix products, per_device(): jnp.dot(head_out, proj_block, preferred_element_type=jnp.float32)  5.18 us
    dot_general x1, matrix products, per_device(): jnp.dot(activation, expert_down[0], preferred_element_type=jnp.float32)  5.06 us
  transfers between devices with their start and end apart: 2, of which 1 were waited for; matrix products, arithmetic and copies ran while one was open for 17% of the time, Pallas kernels for 0%

profile of v1, /device:TPU:0, one launch (start us, length us, event | category | flops | bytes accessed | tf_op | source)
XLA Modules:
  0.0 176.7 jit_solution(10190324230425089868)
XLA Ops:
  0.0 3.0 %collective-permute-start = (bf16[2,512,128]{2,1,0:T(8,128)(2,1)}, bf16[2,512,128]{2,1,0:T(8,128)(2,1)S(1)}, u32[]{:S(2)}, u32[]{:S(2)}) collective-permute-start(bf16[2,512,128]{2,1,0:T(8,128)(2,1)} %bitcast.90), channel_id=1, source_target_pairs={{0,2},{1,3},{2,0},{3,1},{4,6},{5,7},{6,4},{7,5},{8,10},{9,11},{10,... | collective-permute-start | bytes 786440 | tf_op jit(solution)/shard_map/ppermute | solution.py:233
  3.7 2.0 %reshape_squeeze.3 = bf16[2,256,4,128]{3,2,1,0:T(4,128)(2,1)} reshape(bf16[1,512,512]{2,1,0:T(8,128)(2,1)} %param.12) | data formatting | bytes 1048576 | tf_op jit(solution)/shard_map/reshape;squeeze | solution.py:265
  5.7 1.2 dynamic_slice.21
  7.6 1.9 %collective-permute-done = bf16[2,512,128]{2,1,0:T(8,128)(2,1)S(1)} collective-permute-done((bf16[2,512,128]{2,1,0:T(8,128)(2,1)}, bf16[2,512,128]{2,1,0:T(8,128)(2,1)S(1)}, u32[]{:S(2)}, u32[]{:S(2)}) %collective-permute-start) | collective-permute-done | bytes 262176 | tf_op jit(solution)/shard_map/ppermute | solution.py:233
  9.5 1.0 broadcast_select_fusion.1
  10.5 0.8 pad_maximum_fusion
  11.3 25.0 %while.14 = (s32[]{:T(128)}, bf16[2,256,4,128]{3,2,1,0:T(4,128)(2,1)}, s32[]{:T(128)}, s32[2]{0:T(128)S(1)}, bf16[2,256,4,128]{3,2,1,0:T(4,128)(2,1)}, /*index=5*/bf16[2,1024,128]{2,1,0:T(8,128)(2,1)}, s32[]{:T(128)}) while((s32[]{:T(128)}, bf16[2,256,4,128]{3,2,1,0:T(4,128)(2,1)}, s32[]{:T(128)}, s32[2]{0:T(128)S(1)}, ...), condition=%wide.region_3.4_spmd.clone.clone, body=%wide.region_0.3_spmd.clone.clone.sunk | while | flops 544084224 | bytes 15227049 | solution.py:285
  13.2 1.0 and_or_fusion.2
  14.2 1.0 constant_dynamic-slice_fusion.3
  15.2 4.5 %fusion.70 = (f32[4,256]{1,0:T(4,128)S(1)}, f32[4,256,1024]{2,1,0:T(8,128)}) fusion(pred[256,1024]{1,0:T(8,128)(4,1)} %and_or_fusion.2, bf16[1,256,4,128]{3,2,1,0:T(4,128)(2,1)S(1)} %constant_dynamic-slice_fusion.3, bf16[2,1024,128]{2,1,0:T(8,128)(2,1)} %get-tuple-element.236), kind=kOutput, calls=%fused_computation.72.clone.1 | convolution fusion | flops 272630784 | bytes 4984832 | tf_op jit(solution)/shard_map/while/body/eval_jaxpr/sub | solution.py:280
  19.7 3.0 %fusion.71 = bf16[1,256,4,128]{3,1,2,0:T(8,128)(2,1)S(1)} fusion(f32[4,256,1024]{2,1,0:T(8,128)} %get-tuple-element.215, f32[4,256]{1,0:T(4,128)S(1)} %get-tuple-element.216, bf16[2,1024,128]{2,1,0:T(8,128)(2,1)} %get-tuple-element.236), kind=kOutput, calls=%fused_computation.13.clone.1 | convolution fusion | flops 270663680 | bytes 4722688 | tf_op jit(solution)/shard_map/while/body/eval_jaxpr/jtp,pd->tjd/dot_general | solution.py:282
  25.7 1.0 and_or_fusion.2
  26.7 1.0 constant_dynamic-slice_fusion.3
  27.7 4.5 %fusion.70 = (f32[4,256]{1,0:T(4,128)S(1)}, f32[4,256,1024]{2,1,0:T(8,128)}) fusion(pred[256,1024]{1,0:T(8,128)(4,1)} %and_or_fusion.2, bf16[1,256,4,128]{3,2,1,0:T(4,128)(2,1)S(1)} %constant_dynamic-slice_fusion.3, bf16[2,1024,128]{2,1,0:T(8,128)(2,1)} %get-tuple-element.236), kind=kOutput, calls=%fused_computation.72.clone.1 | convolution fusion | flops 272630784 | bytes 4984832 | tf_op jit(solution)/shard_map/while/body/eval_jaxpr/sub | solution.py:280
  32.2 3.0 %fusion.71 = bf16[1,256,4,128]{3,1,2,0:T(8,128)(2,1)S(1)} fusion(f32[4,256,1024]{2,1,0:T(8,128)} %get-tuple-element.215, f32[4,256]{1,0:T(4,128)S(1)} %get-tuple-element.216, bf16[2,1024,128]{2,1,0:T(8,128)(2,1)} %get-tuple-element.236), kind=kOutput, calls=%fused_computation.13.clone.1 | convolution fusion | flops 270663680 | bytes 4722688 | tf_op jit(solution)/shard_map/while/body/eval_jaxpr/jtp,pd->tjd/dot_general | solution.py:282
  36.3 5.2 %convolution_convert_fusion = bf16[512,2048]{1,0:T(8,128)(2,1)} fusion(bf16[256,2048]{1,0:T(8,128)(2,1)} %param.15, bf16[256,2048]{1,0:T(8,128)(2,1)} %collective-permute-done.1, pred[]{:T(512)S(6)} %eq.25, bf16[64,8,4,128]{3,2,1,0:T(4,128)(2,1)} %bitcast.94), kind=kOutput, calls=%fused_computation.38 | convolution fusion | flops 1084227584 | bytes 4718593 | tf_op jit(solution)/shard_map/dot_general | solution.py:295
  41.5 38.6 %shard_map.100 = f32[64,2048]{1,0:T(8,128)} custom-call(bf16[8,64,2048]{2,1,0:T(8,128)(2,1)} %bitcast.89), custom_call_target="tpu_custom_call" | custom-call | tf_op jit(solution)/shard_map/pallas_call | solution.py:125
  80.1 1.2 fusion.43
  83.0 32.6 %shard_map.101 = (bf16[16,64,2048]{2,1,0:T(8,128)(2,1)}, f32[16,16,128]{2,1,0:T(8,128)}) custom-call(bf16[64,2048]{1,0:T(8,128)(2,1)} %copy-done.1, f32[16,128]{1,0:T(8,128)} %pad.4.g_ref), custom_call_target="tpu_custom_call" | custom-call | tf_op jit(solution)/shard_map/pallas_call | solution.py:207
  115.6 0.9 constant_dynamic-slice_fusion.1
  116.5 10.0 %fusion.30 = f32[1024,1536]{1,0:T(8,128)S(1)} fusion(bf16[1024,2048]{1,0:T(8,128)(2,1)} %bitcast.93, bf16[1,2048,1536]{2,1,0:T(8,128)(2,1)} %param.20), kind=kOutput, calls=%fused_computation.33 | convolution fusion | flops 6442450944 | bytes 16777216 | tf_op jit(solution)/shard_map/dot_general | solution.py:320
  126.5 5.1 %multiply_convert_fusion = bf16[1024,2048]{1,0:T(8,128)(2,1)} fusion(f32[1024]{0:T(1024)S(1)} %mul.52, bf16[1,768,2048]{2,1,0:T(8,128)(2,1)S(1)} %copy-done, f32[1024,1536]{1,0:T(8,128)S(1)} %fusion.30), kind=kOutput, calls=%fused_computation.32 | convolution fusion | flops 3230138368 | bytes 13635584 | tf_op jit(solution)/shard_map/dot_general | solution.py:322
  131.6 43.3 %shard_map.102 = f32[64,2048]{1,0:T(8,128)} custom-call(bf16[16,64,2048]{2,1,0:T(8,128)(2,1)} %bitcast.88), custom_call_target="tpu_custom_call" | custom-call | tf_op jit(solution)/shard_map/pallas_call | solution.py:125
  174.9 1.8 %fusion.50 = bf16[1,64,2048]{2,1,0:T(8,128)(2,1)} fusion(f32[64,2048]{1,0:T(8,128)} %shard_map.102, bf16[64,2048]{1,0:T(8,128)(2,1)S(1)} %copy-done.3), kind=kLoop, calls=%fused_computation.61 | loop fusion | flops 393216 | bytes 1048576 | tf_op jit(solution)/shard_map/broadcast_in_dim | solution.py:326
  (42 shorter events, 8.9 us)
Async XLA Ops:
  0.0 126.5 %copy-start = (bf16[1,768,2048]{2,1,0:T(8,128)(2,1)S(1)}, bf16[1,768,2048]{2,1,0:T(8,128)(2,1)}, u32[]{:S(2)}) copy-start(bf16[1,768,2048]{2,1,0:T(8,128)(2,1)} %param.21) | copy-start | bytes 9437188
  0.0 9.5 %collective-permute-start = (bf16[2,512,128]{2,1,0:T(8,128)(2,1)}, bf16[2,512,128]{2,1,0:T(8,128)(2,1)S(1)}, u32[]{:S(2)}, u32[]{:S(2)}) collective-permute-start(bf16[2,512,128]{2,1,0:T(8,128)(2,1)} %bitcast.90), channel_id=1, source_target_pairs={{0,2},{1,3},{2,0},{3,1},{4,6},{5,7},{6,4},{7,5},{8,10},{9,11},{10,... | collective-permute-start | bytes 786440 | tf_op jit(solution)/shard_map/ppermute | solution.py:233
  3.0 33.3 %collective-permute-start.1 = (bf16[256,2048]{1,0:T(8,128)(2,1)}, bf16[256,2048]{1,0:T(8,128)(2,1)}, u32[]{:S(2)}, u32[]{:S(2)}) collective-permute-start(bf16[256,2048]{1,0:T(8,128)(2,1)} %param.15), channel_id=1, source_target_pairs={{0,1},{1,0},{2,3},{3,2},{4,5},{5,4},{6,7},{7,6},{8,9},{9,8},{10,11... | collective-permute-start | bytes 3145736 | tf_op jit(solution)/shard_map/ppermute | solution.py:233
  19.7 3.0 %copy-start.6 = (bf16[2,256,4,128]{3,2,1,0:T(4,128)(2,1)S(1)}, bf16[2,256,4,128]{3,2,1,0:T(4,128)(2,1)}, u32[]{:S(2)}) copy-start(bf16[2,256,4,128]{3,2,1,0:T(4,128)(2,1)} %get-tuple-element.225) | copy-start | bytes 1572868 | tf_op jit(solution)/shard_map/while
  23.0 0.8 copy-start.7
  32.2 3.0 %copy-start.6 = (bf16[2,256,4,128]{3,2,1,0:T(4,128)(2,1)S(1)}, bf16[2,256,4,128]{3,2,1,0:T(4,128)(2,1)}, u32[]{:S(2)}) copy-start(bf16[2,256,4,128]{3,2,1,0:T(4,128)(2,1)} %get-tuple-element.225) | copy-start | bytes 1572868 | tf_op jit(solution)/shard_map/while
  35.5 0.8 copy-start.7
  36.3 43.8 %copy-start.4 = (bf16[1,64,2048]{2,1,0:T(8,128)(2,1)S(1)}, bf16[1,64,2048]{2,1,0:T(8,128)(2,1)}, u32[]{:S(2)}) copy-start(bf16[1,64,2048]{2,1,0:T(8,128)(2,1)} %param.16) | copy-start | bytes 786436
  41.5 40.7 %copy-start.5 = (bf16[2048,16]{0,1:T(8,128)(2,1)S(1)}, bf16[2048,16]{0,1:T(8,128)(2,1)}, u32[]{:S(2)}) copy-start(bf16[2048,16]{0,1:T(8,128)(2,1)} %param.18) | copy-start | bytes 196612
  81.3 0.7 copy-start.2
  82.2 0.8 copy-start.1
  131.6 43.3 %copy-start.3 = (bf16[64,2048]{1,0:T(8,128)(2,1)S(1)}, bf16[64,2048]{1,0:T(8,128)(2,1)}, u32[]{:S(2)}) copy-start(bf16[64,2048]{1,0:T(8,128)(2,1)} %copy-done.2) | copy-start | bytes 786436

commit v2 on v1

--- a/solution.py
+++ b/solution.py
@@ -10,12 +10,8 @@
 
 HEAD_DIM = 128
 FF = 768
-TOP = 8
 TOK_DEV = 64
-CTX = 512
 GROUP = 8
-QH = 4
-SPAN = 512
 EPSILON = 1e-06
 MESH = pl.DeviceIdType.MESH
 
@@ -60,8 +56,8 @@
 
     copies = []
 
-    def send(step):
-        for number in range(1 << (k - 1 - step)):
+    def send(step, only=None):
+        for number in reversed(range(1 << (k - 1 - step))) if only is None else [only]:
             slot = first[step] + number
             flips = [order[step]] + subset(order[step + 1 :], number)
             block = block_of(flips)
@@ -115,6 +111,161 @@
             send(step)
     for _, finish in runs:
         finish(o_ref)
+
+
+def attend_block(block, length, q_ref, halves, rows):
+    heads = q_ref.shape[1] // HEAD_DIM
+    picked = pl.ds(pl.multiple_of(block * rows, rows), rows)
+    query = jnp.concatenate(
+        [q_ref[picked, head * HEAD_DIM : (head + 1) * HEAD_DIM] for head in range(heads)], axis=0
+    )
+    scale = 1.0 / math.sqrt(HEAD_DIM)
+    contract = (((1,), (1,)), ((), ()))
+    old = lax.dot_general(query, halves[0, 0], contract, preferred_element_type=jnp.float32) * scale
+    new = lax.dot_general(query, halves[1, 0], contract, preferred_element_type=jnp.float32) * scale
+    column = lax.broadcasted_iota(jnp.int32, (1, old.shape[1]), 1)
+    old = jnp.where(column < length, old, -1e30)
+    column = lax.broadcasted_iota(jnp.int32, (rows, new.shape[1]), 1)
+    token = lax.broadcasted_iota(jnp.int32, (rows, new.shape[1]), 0) + block * rows
+    bias = jnp.where(column <= token, 0.0, -1e30)
+    new = new + jnp.concatenate([bias] * heads, axis=0)
+    top = jnp.maximum(jnp.max(old, axis=1, keepdims=True), jnp.max(new, axis=1, keepdims=True))
+    old = jnp.exp(old - top)
+    new = jnp.exp(new - top)
+    total = jnp.sum(old, axis=1, keepdims=True) + jnp.sum(new, axis=1, keepdims=True)
+    mixed = jnp.dot(old.astype(jnp.bfloat16), halves[0, 1], preferred_element_type=jnp.float32)
+    mixed += jnp.dot(new.astype(jnp.bfloat16), halves[1, 1], preferred_element_type=jnp.float32)
+    mixed = (mixed / total).astype(jnp.bfloat16)
+    return jnp.concatenate(
+        [mixed[head * rows : (head + 1) * rows] for head in range(heads)], axis=1
+    )
+
+
+def attention_kernel(
+    unit, parts, bits,
+    lengths_ref, q_ref, kv_ref, proj_ref, o_ref,
+    halves, proj, heads, x, recv, stage,
+    send_sem, recv_sem, kv_sem, proj_send, proj_recv, own_sem,
+):
+    me = lax.axis_index("dev")
+    low = list(range(unit))
+    mates = [flipped(me, subset(low, number)) for number in range(1, 1 << unit)]
+    ranks = [flipped(me, [unit + bit]) for bit in bits]
+    barrier = pltpu.get_barrier_semaphore()
+    for other in mates + ranks:
+        pl.semaphore_signal(barrier, inc=1, device_id={"dev": other}, device_id_type=MESH)
+    request = me % (1 << unit)
+    rank = me // (1 << unit)
+    parity = rank % 2
+    depth = proj_ref.shape[0]
+    own_rows = pl.ds(pl.multiple_of(request * depth, depth), depth)
+    own_half = pltpu.make_async_copy(kv_ref, halves.at[parity], own_sem.at[0])
+    own_proj = pltpu.make_async_copy(proj_ref, proj.at[own_rows], own_sem.at[1])
+    own_half.start()
+    own_proj.start()
+    pl.semaphore_wait(barrier, len(mates) + len(ranks))
+    kv_copy = pltpu.make_async_remote_copy(
+        src_ref=kv_ref,
+        dst_ref=halves.at[parity],
+        send_sem=kv_sem.at[0],
+        recv_sem=kv_sem.at[1],
+        device_id={"dev": ranks[0]},
+        device_id_type=MESH,
+    )
+    kv_copy.start()
+    proj_copies = []
+    for place, other in enumerate(mates):
+        copy = pltpu.make_async_remote_copy(
+            src_ref=proj_ref,
+            dst_ref=proj.at[own_rows],
+            send_sem=proj_send.at[place],
+            recv_sem=proj_recv.at[place],
+            device_id={"dev": other},
+            device_id_type=MESH,
+        )
+        copy.start()
+        proj_copies.append(copy)
+    own_half.wait()
+    kv_copy.wait()
+
+    blocks, rows, width = x.shape
+    far = 1 << (len(bits) - 1)
+    masks = sorted(range(blocks), key=lambda m: (-bin(m).count("1"), -(m & far), m))
+    place_of = {mask: place for place, mask in enumerate(masks)}
+    length = lengths_ref[request]
+    runs = [
+        scatter_steps(
+            me, unit, number, order, cols, x, recv, stage, send_sem, recv_sem,
+            lambda flips: place_of[sum(1 << bit for bit in flips)],
+        )
+        for number, (order, cols) in enumerate(parts)
+    ]
+    half = blocks // 2
+    strip = math.gcd(width, 512)
+    for group in range(2):
+        for spot in range(half):
+            mask = masks[group * half + spot]
+            block = flipped(rank, subset(bits, mask))
+            heads[spot * rows : (spot + 1) * rows, :] = attend_block(
+                block, length, q_ref, halves, rows
+            )
+        if group == 0:
+            own_proj.wait()
+            for copy in proj_copies:
+                copy.wait()
+        for start in range(0, width, strip):
+            product = jnp.dot(
+                heads[...], proj[:, start : start + strip], preferred_element_type=jnp.float32
+            ).astype(x.dtype)
+            for spot in range(half):
+                x[group * half + spot, :, start : start + strip] = product[
+                    spot * rows : (spot + 1) * rows
+                ]
+        for spot in range(half):
+            mask = masks[group * half + spot]
+            for (send, _), (order, _) in zip(runs, parts):
+                if mask >> order[0] & 1:
+                    number = sum((mask >> bit & 1) << at for at, bit in enumerate(order[1:]))
+                    send(0, number)
+    for step in range(1, len(bits)):
+        for send, _ in runs:
+            send(step)
+    for _, finish in runs:
+        finish(o_ref)
+
+
+def attention(lengths, queries, key_values, out_proj, unit, orders, collective_id):
+    width = out_proj.shape[1]
+    tokens, columns = queries.shape
+    bits = sorted(orders[0])
+    blocks = 1 << len(bits)
+    rows = tokens // blocks
+    cut = width * 3 // 4 // 128 * 128
+    parts = [(orders[0], pl.ds(0, cut)), (orders[1], pl.ds(cut, width - cut))]
+    mates = max((1 << unit) - 1, 1)
+    kind = queries.dtype
+    whole = pl.BlockSpec(memory_space=pltpu.VMEM)
+    return pl.pallas_call(
+        functools.partial(attention_kernel, unit, parts, bits),
+        out_shape=jax.ShapeDtypeStruct((rows, width), jnp.float32),
+        in_specs=[pl.BlockSpec(memory_space=pltpu.SMEM), whole, whole, whole],
+        out_specs=whole,
+        scratch_shapes=[
+            pltpu.VMEM((2,) + key_values.shape, kind),
+            pltpu.VMEM((out_proj.shape[0] << unit, width), kind),
+            pltpu.VMEM((tokens // 2, columns), kind),
+            pltpu.VMEM((blocks, rows, width), kind),
+            pltpu.VMEM((blocks - 1, rows, width), kind),
+            pltpu.VMEM((max(blocks // 2 - 1, 1), rows, width), kind),
+            pltpu.SemaphoreType.DMA((2, blocks - 1)),
+            pltpu.SemaphoreType.DMA((2, blocks - 1)),
+            pltpu.SemaphoreType.DMA((2,)),
+            pltpu.SemaphoreType.DMA((mates,)),
+            pltpu.SemaphoreType.DMA((mates,)),
+            pltpu.SemaphoreType.DMA((2,)),
+        ],
+        compiler_params=pltpu.CompilerParams(collective_id=collective_id, has_side_effects=True),
+    )(lengths, queries, key_values, out_proj)
 
 
 def reduce_scatter(x, unit, orders, collective_id):
@@ -227,12 +378,6 @@
     return order
 
 
-def partner(block, axis, stride):
-    count = lax.axis_size(axis)
-    route = [(i, i ^ 1 << stride) for i in range(count)]
-    return lax.ppermute(block, axis, route)
-
-
 def per_device(
     queries,
     key_values,
@@ -250,52 +395,10 @@
     width = residual.shape[-1]
     requests_n = devices // GROUP
     low_bits = bit_count(requests_n)
-    tp_rank = my_index // requests_n
-    request = my_index % requests_n
-    is_upper = tp_rank % 2 == 1
-    own_half = key_values[:, 0]
-    other_half = partner(own_half, "dev", low_bits)
-    first_part = jnp.where(is_upper, other_half, own_half)
-    second_part = jnp.where(is_upper, own_half, other_half)
-    key_seq = jnp.concatenate([first_part, second_part], axis=1)
-    length = lengths[request]
-    positions = jnp.arange(CTX + SPAN, dtype=jnp.int32)
-    qblock = math.gcd(SPAN, 256)
-    score_scale = 1.0 / math.sqrt(HEAD_DIM)
-    block_queries = queries[0].reshape(SPAN // qblock, qblock, QH, HEAD_DIM)
-    starts = jnp.arange(SPAN // qblock, dtype=jnp.int32) * qblock
-
-    def attend(element):
-        block_q, start = element
-        scores = (
-            jnp.einsum("tjd,pd->jtp", block_q, key_seq[0], preferred_element_type=jnp.float32)
-            * score_scale
-        )
-        row_ids = start + jnp.arange(qblock, dtype=jnp.int32)
-        visible = (positions[None, :] < length) | (positions[None, :] >= CTX) & (
-            positions[None, :] - CTX <= row_ids[:, None]
-        )
-        scores = jnp.where(visible[None], scores, -jnp.inf)
-        row_max = jnp.max(scores, axis=-1, keepdims=True)
-        raised = jnp.exp(scores - row_max)
-        weights = (raised / jnp.sum(raised, axis=-1, keepdims=True)).astype(jnp.bfloat16)
-        mixture = jnp.einsum("jtp,pd->tjd", weights, key_seq[1], preferred_element_type=jnp.float32)
-        return mixture.astype(jnp.bfloat16)
-
-    head_out = lax.map(attend, (block_queries, starts)).reshape(SPAN, QH * HEAD_DIM)
-    proj_block = out_proj
-    for bit_no in range(low_bits):
-        arrived = partner(proj_block, "dev", bit_no)
-        is_high = my_index >> bit_no & 1 == 1
-        proj_block = jnp.where(
-            is_high,
-            jnp.concatenate([arrived, proj_block], axis=0),
-            jnp.concatenate([proj_block, arrived], axis=0),
-        )
-    partial_value = jnp.dot(head_out, proj_block, preferred_element_type=jnp.float32)
-    pieces = partial_value.astype(jnp.bfloat16).reshape(GROUP, TOK_DEV, width)
     near = list(range(bit_count(GROUP)))
-    attended = reduce_scatter(pieces, low_bits, [near, swapped(near, 0, 1)], 1)
+    attended = attention(
+        lengths, queries[0], key_values[:, 0], out_proj, low_bits, [near, swapped(near, 0, 1)], 1
+    )
     stream = (residual[0].astype(jnp.float32) + attended).astype(jnp.bfloat16)
     values = stream.astype(jnp.float32)
     normed = (

time: 177 us -> 134 us (0.76)
  matrix products: 35.5 us -> 16.2 us
  local copies, waits for them, and re-layouts: 10.8 us -> 2.25 us
  other arithmetic: 10.9 us -> 4.87 us
  Pallas kernels: 114 us -> 110 us
  starting transfers between devices: 3 us -> 0 us
  waiting for transfers between devices: 1.87 us -> 0 us
    pallas_call x2 -> x1, Pallas kernels: 81.9 us -> 34.4 us  [reduce_scatter(): pl.pallas_call(functools.partial(scatter_kernel, unit, parts, bits), out_...]
    pallas_call x0 -> x1, Pallas kernels: none -> 43.1 us  [attention(): pl.pallas_call(functools.partial(attention_kernel, unit, parts, bits), ou...]
    dot_general x3 -> x0, matrix products: 11.2 us -> none  [the longest x2 6.06 us: attend(): jnp.einsum('jtp,pd->tjd', weights, key_seq[1], preferred_element_type=jnp...]
    sub x2 -> x0, matrix products: 9 us -> none  [attend(): raised = jnp.exp(scores - row_max)]
    dynamic_slice x5 -> x0, local copies, waits for them, and re-layouts: 4.5 us -> none  [the longest x4 3.25 us: per_device(): lax.map(attend, (block_queries, starts)).reshape(SPAN, QH * HEAD_DIM)]
    ppermute x2 -> x0, starting transfers between devices: 3 us -> none  [partner(): return lax.ppermute(block, axis, route)]
    another operation x1 -> x0, local copies, waits for them, and re-layouts: 1.99 us -> none  [per_device(): block_queries = queries[0].reshape(SPAN // qblock, qblock, QH, HEAD_DIM)]
    or x2 -> x0, other arithmetic: 1.95 us -> none  [attend(): (positions[None, :] < length) | (positions[None, :] >= CTX) & (positions[...]
  transfers between devices with their start and end apart: 2 -> 0, of which waited for: 1 -> 0; matrix products, arithmetic and copies ran while one was open for 17% -> 0% of each run, Pallas kernels for 0% -> 0%
where the time goes in v2:
time: 134 us
  Pallas kernels  110 us (82%)
  matrix products  16.2 us (12%)
  other arithmetic  4.87 us (4%)
  local copies, waits for them, and re-layouts  2.25 us (2%)
    pallas_call x1, Pallas kernels, attention(): pl.pallas_call(functools.partial(attention_kernel, unit, parts, bits), ou...  43.1 us
    pallas_call x1, Pallas kernels, reduce_scatter(): pl.pallas_call(functools.partial(scatter_kernel, unit, parts, bits), out_...  34.4 us
    pallas_call x1, Pallas kernels, all_gather(): pl.pallas_call(functools.partial(gather_kernel, parts, bits), out_shape=[...  32.7 us
    dot_general x1, matrix products, per_device(): jnp.dot(flat_rows, expert_gate_up[0], preferred_element_type=jnp.float32)  10 us
    dot_general x1, matrix products, per_device(): jnp.dot(activation, expert_down[0], preferred_element_type=jnp.float32)  5.05 us

profile of v2, /device:TPU:0, one launch (start us, length us, event | category | flops | bytes accessed | tf_op | source)
XLA Modules:
  0.0 133.6 jit_solution(811252687695542961)
XLA Ops:
  0.0 0.0 copy-start
  0.0 0.9 fusion.13
  0.9 0.8 convert_element_type.33
  1.7 43.1 %shard_map.100 = f32[64,2048]{1,0:T(8,128)} custom-call(s32[2]{0:T(128)} %lengths_ref.1, bf16[512,512]{1,0:T(8,128)(2,1)} %bitcast.25, bf16[2,512,128]{2,1,0:T(8,128)(2,1)} %bitcast.26, bf16[256,2048]{1,0:T(8,128)(2,1)} %proj_ref.1), custom_call_target="tpu_custom_call" | custom-call | tf_op jit(solution)/shard_map/pallas_call | solution.py:248
  44.8 1.3 fusion.7
  46.1 0.0 copy-start.2
  46.1 0.7 copy-done.2
  46.8 0.1 fusion.9.x_ref
  46.9 0.0 copy-start.1
  46.9 1.1 fusion.16
  48.1 0.6 pad.4.g_ref
  48.7 0.0 copy-done.1
  48.7 32.7 %shard_map.101 = (bf16[16,64,2048]{2,1,0:T(8,128)(2,1)}, f32[16,16,128]{2,1,0:T(8,128)}) custom-call(bf16[64,2048]{1,0:T(8,128)(2,1)} %copy-done.1, f32[16,128]{1,0:T(8,128)} %pad.4.g_ref), custom_call_target="tpu_custom_call" | custom-call | tf_op jit(solution)/shard_map/pallas_call | solution.py:358
  81.4 0.9 constant_dynamic-slice_fusion
  82.2 0.1 mul.41
  82.3 10.0 %fusion = f32[1024,1536]{1,0:T(8,128)S(1)} fusion(bf16[1024,2048]{1,0:T(8,128)(2,1)} %bitcast.29, bf16[1,2048,1536]{2,1,0:T(8,128)(2,1)} %param.18), kind=kOutput, calls=%fused_computation.1 | convolution fusion | flops 6442450944 | bytes 16777216 | tf_op jit(solution)/shard_map/dot_general | solution.py:423
  92.3 0.0 copy-done
  92.3 5.0 %multiply_convert_fusion = bf16[1024,2048]{1,0:T(8,128)(2,1)} fusion(f32[1024]{0:T(1024)S(1)} %mul.41, bf16[1,768,2048]{2,1,0:T(8,128)(2,1)S(1)} %copy-done, f32[1024,1536]{1,0:T(8,128)S(1)} %fusion), kind=kOutput, calls=%fused_computation | convolution fusion | flops 3230138368 | bytes 13635584 | tf_op jit(solution)/shard_map/dot_general | solution.py:425
  97.4 0.0 copy-start.3
  97.4 34.4 %shard_map.102 = f32[64,2048]{1,0:T(8,128)} custom-call(bf16[16,64,2048]{2,1,0:T(8,128)(2,1)} %bitcast.24), custom_call_target="tpu_custom_call" | custom-call | tf_op jit(solution)/shard_map/pallas_call | solution.py:276
  131.8 0.0 copy-done.3
  131.8 1.8 %fusion.12 = bf16[1,64,2048]{2,1,0:T(8,128)(2,1)} fusion(f32[64,2048]{1,0:T(8,128)} %shard_map.102, bf16[64,2048]{1,0:T(8,128)(2,1)S(1)} %copy-done.3), kind=kLoop, calls=%fused_computation.18 | loop fusion | flops 393216 | bytes 1048576 | tf_op jit(solution)/shard_map/broadcast_in_dim | solution.py:429
  (2 shorter events, 0.0 us)
Async XLA Ops:
  0.0 92.3 %copy-start = (bf16[1,768,2048]{2,1,0:T(8,128)(2,1)S(1)}, bf16[1,768,2048]{2,1,0:T(8,128)(2,1)}, u32[]{:S(2)}) copy-start(bf16[1,768,2048]{2,1,0:T(8,128)(2,1)} %param.19) | copy-start | bytes 9437188
  46.1 0.7 copy-start.2
  46.9 1.8 %copy-start.1 = (bf16[64,2048]{1,0:T(8,128)(2,1)}, bf16[64,2048]{1,0:T(8,128)(2,1)S(1)}, u32[]{:S(2)}) copy-start(bf16[64,2048]{1,0:T(8,128)(2,1)S(1)} %fusion.9.x_ref) | copy-start | bytes 786436
  97.4 34.5 %copy-start.3 = (bf16[64,2048]{1,0:T(8,128)(2,1)S(1)}, bf16[64,2048]{1,0:T(8,128)(2,1)}, u32[]{:S(2)}) copy-start(bf16[64,2048]{1,0:T(8,128)(2,1)} %copy-done.2) | copy-start | bytes 786436
